TPU v7x, 256 devices: a whole 4x4x8 slice. The times are simulated.
256 devices in a mesh: pop: 64 (over z, y, core), tp: 4 (over x).
Axes of the slice: x: 4, y: 4, z: 8, core: 2. Of those that a mesh axis runs over, the one named last changes fastest.
Arguments:
- tokens: bfloat16 [65536, 5120], P('pop', 'tp'), may hold values from -6 to 6
- target: bfloat16 [65536, 5120], P('pop', 'tp'), may hold values from -6 to 6
- weight: bfloat16 [5120, 5120], P('pop', 'tp'), may hold values from -6 to 6
- factor_out: bfloat16 [256, 4, 5120], P('pop'), may hold values from -6 to 6
- factor_in: bfloat16 [256, 4, 5120], P('pop', None, 'tp'), may hold values from -6 to 6
Outputs:
- perturbed: bfloat16 [65536, 5120], P('pop', 'tp')
- new_weight: bfloat16 [5120, 5120], P('pop', 'tp')
All inputs are finite; a program needn't handle non-finite values.
Results may differ from a plain program's by a relative error of at most 0.012.
Values may be sent and summed in bfloat16 or wider, within the bound.
A program may use at most 128 MiB of HBM per device.

v0:
```python
import math
import jax
import jax.numpy as jnp
from jax import lax
from jax.sharding import PartitionSpec as P

noise_scale = 0.25
step_scale = 10.0


def sent_to_all(shard, axis):
    count = lax.axis_size(axis)
    return lax.all_to_all(
        jnp.broadcast_to(shard[None], (count, *shard.shape)), axis, 0, 0, tiled=True
    )


def taken_together(shard, axis):
    everything = sent_to_all(shard, axis)
    return jnp.sum(everything, axis=0)


def local(tokens, target, weight, factor_out, factor_in):
    tok_rows, shard_width = tokens.shape
    mem_local, rank, width_out = factor_out.shape
    tok_member = tok_rows // mem_local
    tp_count = lax.axis_size("tp")
    width_in = shard_width * tp_count
    out_cols = width_out // tp_count
    col_first = lax.axis_index("tp") * out_cols
    base_factor = 1.0 / math.sqrt(width_in)
    token_sets = tokens.reshape(mem_local, tok_member, shard_width)
    codes_part = jnp.einsum(
        "mkc,mrc->mkr", token_sets, factor_in, preferred_element_type=jnp.float32
    )
    codes_sum = taken_together(codes_part, "tp")
    partial_terms = (
        lax.dot_general(
            tokens,
            lax.all_gather(weight, "pop", axis=0, tiled=True),
            (((1,), (1,)), ((), ())),
            preferred_element_type=jnp.float32,
        )
        * base_factor
    )
    base_sum = lax.psum_scatter(
        partial_terms.astype(jnp.bfloat16), "tp", scatter_dimension=1, tiled=True
    ).astype(jnp.float32)
    outer_cols = lax.dynamic_slice_in_dim(factor_out, col_first, out_cols, 2).astype(jnp.float32)
    low_rank = jnp.einsum(
        "mkr,mrc->mkc", codes_sum, outer_cols, precision=lax.Precision.HIGHEST
    ) * (noise_scale / math.sqrt(rank * width_in))
    output_full = base_sum.reshape(mem_local, tok_member, out_cols) + low_rank
    wanted = target.reshape(mem_local, tok_member, out_cols).astype(jnp.float32)
    fitness_part = jnp.sum(output_full * wanted, axis=(1, 2)) / (tok_member * math.sqrt(width_out))
    fitness_grid = lax.all_gather(fitness_part[None, :], ("pop", "tp"), axis=0, tiled=True)
    fitness_all = jnp.sum(fitness_grid.reshape(-1, tp_count, mem_local), axis=1).reshape(-1)
    outer_rows = lax.all_to_all(factor_out, "pop", split_axis=2, concat_axis=0, tiled=True)
    inner_cols = lax.all_gather(factor_in, "pop", axis=0, tiled=True)
    centered = fitness_all - jnp.mean(fitness_all)
    scaled = (centered[:, None, None] * outer_rows.astype(jnp.float32)).astype(jnp.bfloat16)
    delta = jnp.einsum("imo,imc->oc", scaled, inner_cols, preferred_element_type=jnp.float32)
    members_all = fitness_all.shape[0]
    updated = (
        weight.astype(jnp.float32) + step_scale / math.sqrt(members_all * rank) * delta
    ).astype(jnp.bfloat16)
    return (output_full.reshape(tok_rows, out_cols).astype(jnp.bfloat16), updated)


def solution(mesh):
    in_specs = (
        P("pop", "tp"),
        P("pop", "tp"),
        P("pop", "tp"),
        P("pop", None, None),
        P("pop", None, "tp"),
    )
    out_specs = (P("pop", "tp"), P("pop", "tp"))
    return jax.shard_map(local, mesh=mesh, in_specs=in_specs, out_specs=out_specs, check_vma=False)
```

profile of v0, /device:TPU:1, one launch (start us, length us, event | category | flops | bytes accessed | tf_op | source)
XLA Modules:
  0.0 318.1 jit_solution(7085557132596609108)
XLA Ops:
  7.2 0.0 copy-start
  7.2 0.0 all-gather.4.cloned.1.call-start
  7.2 0.7 all-gather.4.cloned.1.call-update
  7.9 0.0 reduce-scatter.2.cloned.1.call-start
  8.0 97.6 %all-gather.4.cloned.1.call-done = bf16[5120,1280]{1,0:T(8,128)(2,1)} async-done(((bf16[80,1280]{1,0:T(8,128)(2,1)}), bf16[5120,1280]{1,0:T(8,128)(2,1)}) %all-gather.4.cloned.1.call-update) | async-done | bytes 13107216 | tf_op jit(solution)/shard_map/all_gather | solution.py:40
  105.5 0.0 copy-done
  105.5 20.6 %multiply_convert_fusion = bf16[1024,5120]{1,0:T(8,128)(2,1)} fusion(bf16[1024,1280]{1,0:T(8,128)(2,1)S(1)} %copy-done, bf16[5120,1280]{1,0:T(8,128)(2,1)} %all-gather.4.cloned.1.call-done), kind=kOutput, calls=%fused_computation | convolution fusion | flops 13432258560 | bytes 26214400 | tf_op jit(solution)/shard_map/dot_general | solution.py:38
  126.1 0.0 reduce-scatter.2.cloned.1.call-update
  126.2 0.0 all-gather.6.cloned.1.call-start
  126.2 0.7 all-gather.6.cloned.1.call-update
  126.9 0.0 copy-done.3
  126.9 0.8 fusion.18
  127.7 0.7 broadcast_in_dim.2
  128.3 4.0 %all-to-all-start = ((f32[4,4,256,4]{2,3,1,0:T(4,128)}), f32[4,4,256,4]{2,3,1,0:T(4,128)S(1)}, u32[]{:S(2)}, u32[]{:S(2)}) async-start(f32[4,4,256,4]{2,3,1,0:T(4,128)} %broadcast_in_dim.2), calls=%async_computation.1 | async-start | bytes 131072 | tf_op jit(solution)/shard_map/all_to_all | solution.py:13
  132.3 5.2 %copy.12 = bf16[4,4,5120]{1,0,2:T(4,128)(2,1)} copy(bf16[4,4,5120]{2,1,0:T(4,128)(2,1)S(1)} %copy-done.2) | data formatting | bytes 327680 | tf_op args[3]
  137.5 11.2 %reshape.57 = bf16[64,2,640]{2,1,0:T(2,128)(2,1)} reshape(bf16[5120,4,4]{2,1,0:T(4,128)(2,1)} %bitcast.28) | data formatting | bytes 327680
  148.7 0.0 all-to-all-done
  148.7 6.4 %all-to-all-start.1 = ((bf16[64,2,640]{2,1,0:T(2,128)(2,1)}), bf16[64,2,640]{2,1,0:T(2,128)(2,1)S(1)}, u32[]{:S(2)}, u32[]{:S(2)}) async-start(bf16[64,2,640]{2,1,0:T(2,128)(2,1)} %reshape.57), calls=%async_computation.2 | async-start | bytes 327680 | tf_op jit(solution)/shard_map/all_to_all | solution.py:58
  155.2 11.6 %all-to-all-done.1 = bf16[64,2,640]{2,1,0:T(2,128)(2,1)S(1)} async-done(((bf16[64,2,640]{2,1,0:T(2,128)(2,1)}), bf16[64,2,640]{2,1,0:T(2,128)(2,1)S(1)}, u32[]{:S(2)}, u32[]{:S(2)}) %all-to-all-start.1) | async-done | bytes 163872 | tf_op jit(solution)/shard_map/all_to_all | solution.py:58
  166.8 12.3 %reshape.58 = bf16[5120,4,4]{2,1,0:T(4,128)(2,1)} reshape(bf16[64,2,640]{2,1,0:T(2,128)(2,1)S(1)} %all-to-all-done.1) | data formatting | bytes 327680
  179.1 6.9 %copy.13 = f32[4,4,64,80]{3,0,2,1:T(4,128)S(1)} copy(bf16[4,4,64,80]{1,0,3,2:T(4,128)(2,1)} %bitcast.27) | data formatting | bytes 491520 | tf_op jit(solution)/shard_map/convert_element_type | solution.py:61
  186.0 0.0 copy-start.1
  186.0 37.5 %reduce-scatter.2.cloned.1.call-done = bf16[1024,1280]{1,0:T(8,128)(2,1)} async-done(((bf16[1024,5120]{1,0:T(8,128)(2,1)}), bf16[1024,1280]{1,0:T(8,128)(2,1)}) %reduce-scatter.2.cloned.1.call-update) | async-done | bytes 2621456 | tf_op jit(solution)/shard_map/reduce_scatter | solution.py:46
  223.4 7.2 %fusion = (f32[4]{0:T(128)S(1)}, bf16[4,256,1280]{2,1,0:T(8,128)(2,1)}) fusion(bf16[4,256,1280]{2,1,0:T(8,128)(2,1)} %bitcast.30, f32[4,256,4]{1,2,0:T(4,128)S(1)} %reduce_sum.36, bf16[4,4,5120]{2,1,0:T(4,128)(2,1)S(1)} %copy-done.2, s32[]{:T(128)S(6)} %select_n.3, bf16[4,256,1280]{2,1,0:T(8,128)(2,1)} %bitcast.31), kind=kOutput, calls=%fused_computation.2 | convolution fusion | flops 72089600 | bytes 7921684 | tf_op jit(solution)/shard_map/mkr,mrc->mkc/dot_general | solution.py:50
  230.6 0.1 multiply_dynamic-update-slice_fusion
  230.7 76.1 %all-reduce = f32[1024]{0:T(1024)S(1)} all-reduce(f32[1024]{0:T(1024)S(1)} %multiply_dynamic-update-slice_fusion), channel_id=2, replica_groups=mesh['pop'=64,'tp'=4] {'pop','tp'}, use_global_device_ids=true, to_apply=%add | all-reduce | flops 1024 | bytes 8192
  306.8 0.6 reduce_sum.39
  307.4 0.2 reshape.46
  307.6 0.1 reduce_sum.38
  308.3 0.1 sub.15
  308.4 0.0 all-gather.6.cloned.1.call-done
  308.5 3.1 fusion.12
  (7 shorter events, 0.0 us)
Async XLA Ops:
  7.2 98.4 %copy-start = (bf16[1024,1280]{1,0:T(8,128)(2,1)S(1)}, bf16[1024,1280]{1,0:T(8,128)(2,1)}, u32[]{:S(2)}) copy-start(bf16[1024,1280]{1,0:T(8,128)(2,1)} %param.5) | copy-start | bytes 7864324
  7.2 98.3 %all-gather.4.cloned.1.call-start = ((), (), s32[]{:S(2)}) async-start(), calls=%async_computation.3 | async-start | bytes 13312000 | tf_op jit(solution)/shard_map/all_gather | solution.py:40
  7.9 215.5 %reduce-scatter.2.cloned.1.call-start = ((), (), s32[]{:S(2)}) async-start(), calls=%async_computation.4 | async-start | bytes 13107200 | tf_op jit(solution)/shard_map/reduce_scatter | solution.py:46
  126.1 0.8 copy-start.3
  126.1 6.2 %copy-start.2 = (bf16[4,4,5120]{2,1,0:T(4,128)(2,1)S(1)}, bf16[4,4,5120]{2,1,0:T(4,128)(2,1)}, u32[]{:S(2)}) copy-start(bf16[4,4,5120]{2,1,0:T(4,128)(2,1)} %param.8) | copy-start | bytes 491524
  126.2 182.3 %all-gather.6.cloned.1.call-start = ((), (), s32[]{:S(2)}) async-start(), calls=%async_computation.5 | async-start | bytes 2662400 | tf_op jit(solution)/shard_map/all_gather | solution.py:59
  128.3 20.4 %all-to-all-start = ((f32[4,4,256,4]{2,3,1,0:T(4,128)}), f32[4,4,256,4]{2,3,1,0:T(4,128)S(1)}, u32[]{:S(2)}, u32[]{:S(2)}) async-start(f32[4,4,256,4]{2,3,1,0:T(4,128)} %broadcast_in_dim.2), calls=%async_computation.1 | async-start | bytes 131072 | tf_op jit(solution)/shard_map/all_to_all | solution.py:13
  148.7 18.1 %all-to-all-start.1 = ((bf16[64,2,640]{2,1,0:T(2,128)(2,1)}), bf16[64,2,640]{2,1,0:T(2,128)(2,1)S(1)}, u32[]{:S(2)}, u32[]{:S(2)}) async-start(bf16[64,2,640]{2,1,0:T(2,128)(2,1)} %reshape.57), calls=%async_computation.2 | async-start | bytes 327680 | tf_op jit(solution)/shard_map/all_to_all | solution.py:58
  186.0 122.5 %copy-start.1 = (bf16[80,1280]{1,0:T(8,128)(2,1)S(1)}, bf16[80,1280]{1,0:T(8,128)(2,1)}, u32[]{:S(2)}) copy-start(bf16[80,1280]{1,0:T(8,128)(2,1)} %param.7) | copy-start | bytes 614404
Sparse Core Ops, SparseCore 0:
  10.7 94.7 all-gather.3
  126.3 97.1 reduce-scatter.1
  226.2 77.3 all-gather.5
where the time goes:
time: 319 us; the launch traced here: 318 us
  waiting for transfers between devices  148 us (46%)
  blocking collectives  76.1 us (24%)
  local copies, waits for them, and re-layouts  36.6 us (11%)
  matrix products  31.7 us (10%)
  between operations  14.5 us (5%)
  starting transfers between devices  10.5 us (3%)
    all_gather x1, waiting for transfers between devices, local(): lax.all_gather(weight, 'pop', axis=0, tiled=True)  97.6 us
    unnamed x1, blocking collectives  76.1 us
    reduce_scatter x1, waiting for transfers between devices, local(): lax.psum_scatter(partial_terms.astype(jnp.bfloat16), 'tp', scatter_dimens...  37.5 us
    unnamed x12, local copies, waits for them, and re-layouts  28.7 us
    dot_general x1, matrix products, local(): lax.dot_general(tokens, lax.all_gather(weight, 'pop', axis=0, tiled=True)...  20.6 us
    all_to_all x1, waiting for transfers between devices, local(): lax.all_to_all(factor_out, 'pop', split_axis=2, concat_axis=0, tiled=True)  11.6 us
    dot_general x1, matrix products, local(): jnp.einsum('mkr,mrc->mkc', codes_sum, outer_cols, precision=lax.Precision...  7.16 us
    convert_element_type x1, local copies, waits for them, and re-layouts, local(): outer_rows.astype(jnp.float32)  6.9 us
  transfers between devices with their start and end apart: 5, of which 3 were waited for; matrix products, arithmetic and copies ran while one was open for 14% of the time, Pallas kernels for 0%

commit v1 on v0

--- a/solution.py
+++ b/solution.py
@@ -37,7 +37,9 @@
     partial_terms = (
         lax.dot_general(
             tokens,
-            lax.all_gather(weight, "pop", axis=0, tiled=True),
+            jnp.concatenate(
+                lax.all_to_all(jnp.stack([weight] * lax.axis_size("pop")), "pop", 0, 0), axis=0
+            ),
             (((1,), (1,)), ((), ())),
             preferred_element_type=jnp.float32,
         )

time: 319 us -> 528 us (1.66)
  blocking collectives: 76.1 us -> 376 us
  waiting for transfers between devices: 148 us -> 49.7 us
  local copies, waits for them, and re-layouts: 36.6 us -> 43.4 us
    all_to_all x0 -> x1, blocking collectives: none -> 301 us  [local(): lax.all_to_all(jnp.stack([weight] * lax.axis_size('pop')), 'pop', 0, 0)]
    all_gather x1 -> x0, waiting for transfers between devices: 97.6 us -> none  [local(): lax.all_gather(weight, 'pop', axis=0, tiled=True)]
    another operation x0 -> x1, local copies, waits for them, and re-layouts: none -> 6.64 us  [local(): jnp.stack([weight] * lax.axis_size('pop'))]
  transfers between devices with their start and end apart: 5 -> 4, of which waited for: 3 -> 2; matrix products, arithmetic and copies ran while one was open for 14% -> 9% of each run, Pallas kernels for 0% -> 0%
where the time goes in v1:
time: 528 us
  blocking collectives  376 us (71%)
  waiting for transfers between devices  49.7 us (9%)
  local copies, waits for them, and re-layouts  43.4 us (8%)
  matrix products  31.7 us (6%)
  between operations  16.2 us (3%)
  starting transfers between devices  9.97 us (2%)
    all_to_all x1, blocking collectives, local(): lax.all_to_all(jnp.stack([weight] * lax.axis_size('pop')), 'pop', 0, 0)  301 us
    unnamed x1, blocking collectives  75.4 us
    reduce_scatter x1, waiting for transfers between devices, local(): lax.psum_scatter(partial_terms.astype(jnp.bfloat16), 'tp', scatter_dimens...  37.3 us
    unnamed x12, local copies, waits for them, and re-layouts  28.9 us
    dot_general x1, matrix products, local(): lax.dot_general(tokens, jnp.concatenate(lax.all_to_all(jnp.stack([weight]...  20.6 us
    all_to_all x1, waiting for transfers between devices, local(): lax.all_to_all(factor_out, 'pop', split_axis=2, concat_axis=0, tiled=True)  11.8 us
  transfers between devices with their start and end apart: 4, of which 2 were waited for; matrix products, arithmetic and copies ran while one was open for 9% of the time, Pallas kernels for 0%

profile of v1, /device:TPU:1, one launch (start us, length us, event | category | flops | bytes accessed | tf_op | source)
XLA Modules:
  0.0 527.8 jit_solution(7769528666398566438)
XLA Ops:
  8.0 0.0 copy-start
  8.0 0.0 reduce-scatter.2.cloned.1.call-start
  8.1 6.6 %stack.2 = bf16[64,80,1280]{2,1,0:T(8,128)(2,1)} broadcast(bf16[80,1280]{1,0:T(8,128)(2,1)} %param.7), dimensions={1,2} | broadcast | bytes 13312000 | tf_op jit(solution)/shard_map/stack | solution.py:41
  14.7 300.7 %all_to_all.19 = bf16[64,80,1280]{2,1,0:T(8,128)(2,1)} all-to-all(bf16[64,80,1280]{2,1,0:T(8,128)(2,1)} %stack.2), channel_id=1, replica_groups=mesh['pop'=64,'tp'=4] {'pop'}, dimensions={0} | all-to-all | bytes 26214400 | tf_op jit(solution)/shard_map/all_to_all | solution.py:41
  315.4 0.0 copy-done
  315.4 20.6 %multiply_convert_fusion = bf16[1024,5120]{1,0:T(8,128)(2,1)} fusion(bf16[1024,1280]{1,0:T(8,128)(2,1)S(1)} %copy-done, bf16[5120,1280]{1,0:T(8,128)(2,1)} %bitcast.30), kind=kOutput, calls=%fused_computation | convolution fusion | flops 13432258560 | bytes 26214400 | tf_op jit(solution)/shard_map/dot_general | solution.py:38
  336.0 0.0 reduce-scatter.2.cloned.1.call-update
  336.0 0.0 all-gather.3.cloned.1.call-start
  336.1 0.5 all-gather.3.cloned.1.call-update
  336.6 0.2 copy-done.3
  336.8 0.8 fusion.18
  337.5 0.7 broadcast_in_dim.2
  338.2 4.0 all-to-all-start.1
  342.2 0.0 copy-done.2
  342.2 5.2 copy.12
  347.4 11.2 %reshape.63 = bf16[64,2,640]{2,1,0:T(2,128)(2,1)} reshape(bf16[5120,4,4]{2,1,0:T(4,128)(2,1)} %bitcast.29) | data formatting | bytes 327680
  358.6 0.0 all-to-all-done.1
  358.7 5.9 %all-to-all-start.2 = ((bf16[64,2,640]{2,1,0:T(2,128)(2,1)}), bf16[64,2,640]{2,1,0:T(2,128)(2,1)S(1)}, u32[]{:S(2)}, u32[]{:S(2)}) async-start(bf16[64,2,640]{2,1,0:T(2,128)(2,1)} %reshape.63), calls=%async_computation.3 | async-start | bytes 327680 | tf_op jit(solution)/shard_map/all_to_all | solution.py:60
  364.6 11.8 %all-to-all-done.2 = bf16[64,2,640]{2,1,0:T(2,128)(2,1)S(1)} async-done(((bf16[64,2,640]{2,1,0:T(2,128)(2,1)}), bf16[64,2,640]{2,1,0:T(2,128)(2,1)S(1)}, u32[]{:S(2)}, u32[]{:S(2)}) %all-to-all-start.2) | async-done | bytes 163872 | tf_op jit(solution)/shard_map/all_to_all | solution.py:60
  376.4 12.3 %reshape.64 = bf16[5120,4,4]{2,1,0:T(4,128)(2,1)} reshape(bf16[64,2,640]{2,1,0:T(2,128)(2,1)S(1)} %all-to-all-done.2) | data formatting | bytes 327680
  388.7 6.9 %copy.13 = f32[4,4,64,80]{3,0,2,1:T(4,128)S(1)} copy(bf16[4,4,64,80]{1,0,3,2:T(4,128)(2,1)} %bitcast.28) | data formatting | bytes 491520 | tf_op jit(solution)/shard_map/convert_element_type | solution.py:63
  395.6 0.0 copy-start.1
  395.6 37.3 %reduce-scatter.2.cloned.1.call-done = bf16[1024,1280]{1,0:T(8,128)(2,1)} async-done(((bf16[1024,5120]{1,0:T(8,128)(2,1)}), bf16[1024,1280]{1,0:T(8,128)(2,1)}) %reduce-scatter.2.cloned.1.call-update) | async-done | bytes 2621456 | tf_op jit(solution)/shard_map/reduce_scatter | solution.py:48
  432.9 7.2 %fusion = (f32[4]{0:T(128)S(1)}, bf16[4,256,1280]{2,1,0:T(8,128)(2,1)}) fusion(bf16[4,256,1280]{2,1,0:T(8,128)(2,1)} %bitcast.32, f32[4,256,4]{1,2,0:T(4,128)S(1)} %reduce_sum.36, bf16[4,4,5120]{2,1,0:T(4,128)(2,1)S(1)} %copy-done.2, s32[]{:T(128)S(6)} %select_n.3, bf16[4,256,1280]{2,1,0:T(8,128)(2,1)} %bitcast.33), kind=kOutput, calls=%fused_computation.2 | convolution fusion | flops 72089600 | bytes 7921684 | tf_op jit(solution)/shard_map/mkr,mrc->mkc/dot_general | solution.py:52
  440.0 0.1 multiply_dynamic-update-slice_fusion
  440.1 75.4 %all-reduce = f32[1024]{0:T(1024)S(1)} all-reduce(f32[1024]{0:T(1024)S(1)} %multiply_dynamic-update-slice_fusion), channel_id=2, replica_groups=mesh['pop'=64,'tp'=4] {'pop','tp'}, use_global_device_ids=true, to_apply=%add | all-reduce | flops 1024 | bytes 8192
  515.5 0.2 reshape.52
  515.7 0.6 reduce_sum.39
  516.3 0.1 reduce_sum.38
  517.1 0.1 sub.15
  517.2 0.0 all-gather.3.cloned.1.call-done
  517.2 3.1 fusion.12
  (6 shorter events, 0.0 us)
Async XLA Ops:
  8.0 307.4 %copy-start = (bf16[1024,1280]{1,0:T(8,128)(2,1)S(1)}, bf16[1024,1280]{1,0:T(8,128)(2,1)}, u32[]{:S(2)}) copy-start(bf16[1024,1280]{1,0:T(8,128)(2,1)} %param.5) | copy-start | bytes 7864324
  8.0 424.9 %reduce-scatter.2.cloned.1.call-start = ((), (), s32[]{:S(2)}) async-start(), calls=%async_computation.4 | async-start | bytes 13107200 | tf_op jit(solution)/shard_map/reduce_scatter | solution.py:48
  336.0 0.8 copy-start.3
  336.0 6.2 %copy-start.2 = (bf16[4,4,5120]{2,1,0:T(4,128)(2,1)S(1)}, bf16[4,4,5120]{2,1,0:T(4,128)(2,1)}, u32[]{:S(2)}) copy-start(bf16[4,4,5120]{2,1,0:T(4,128)(2,1)} %param.8) | copy-start | bytes 491524
  336.0 181.2 %all-gather.3.cloned.1.call-start = ((), (), s32[]{:S(2)}) async-start(), calls=%async_computation.5 | async-start | bytes 2662400 | tf_op jit(solution)/shard_map/all_gather | solution.py:61
  338.2 20.4 %all-to-all-start.1 = ((f32[4,4,256,4]{2,3,1,0:T(4,128)}), f32[4,4,256,4]{2,3,1,0:T(4,128)S(1)}, u32[]{:S(2)}, u32[]{:S(2)}) async-start(f32[4,4,256,4]{2,3,1,0:T(4,128)} %broadcast_in_dim.2), calls=%async_computation.2 | async-start | bytes 131072 | tf_op jit(solution)/shard_map/all_to_all | solution.py:13
  358.7 17.7 %all-to-all-start.2 = ((bf16[64,2,640]{2,1,0:T(2,128)(2,1)}), bf16[64,2,640]{2,1,0:T(2,128)(2,1)S(1)}, u32[]{:S(2)}, u32[]{:S(2)}) async-start(bf16[64,2,640]{2,1,0:T(2,128)(2,1)} %reshape.63), calls=%async_computation.3 | async-start | bytes 327680 | tf_op jit(solution)/shard_map/all_to_all | solution.py:60
  395.6 121.7 %copy-start.1 = (bf16[80,1280]{1,0:T(8,128)(2,1)S(1)}, bf16[80,1280]{1,0:T(8,128)(2,1)}, u32[]{:S(2)}) copy-start(bf16[80,1280]{1,0:T(8,128)(2,1)} %param.7) | copy-start | bytes 614404
Sparse Core Ops, SparseCore 0:
  336.1 96.6 reduce-scatter.1
Sparse Core Ops, SparseCore 1:
  339.2 74.4 all-gather.2
